TPU v7x, 32 devices: a whole 2x2x4 slice. The times are simulated.
32 devices in a mesh: batch: 8 (over y, x, core), seq: 4 (over z).
Axes of the slice: x: 2, y: 2, z: 4, core: 2. Of those that a mesh axis runs over, the one named last changes fastest.
Arguments:
- queries: bfloat16 [8, 2048, 1280], P('batch', 'seq'), may hold values from -120 to 120
- keys: bfloat16 [8, 2048, 1280], P('batch', 'seq'), may hold values from -7.5 to 7.5
- values: bfloat16 [8, 2048, 1280], P('batch', 'seq'), may hold values from -6 to 6
- residual_in: bfloat16 [8, 2048, 1280], P('batch', 'seq'), may hold values from -3 to 3
- w_out: bfloat16 [1280, 1280], replicated, may hold values from -0.15625 to 0.15625
- ln_gain: float32 [1280], replicated, may hold values from 0.5 to 1.5
- w_proj: bfloat16 [1280, 1024], replicated, may hold values from -0.15625 to 0.15625
- texts: float32 [8, 1024], P('batch', 'seq'), may hold values from -1200 to 1200
- labels: int32 [8], replicated, may hold values from 0 to 7, each once
Outputs:
- hidden_out: bfloat16 [8, 2048, 1280], P('batch', 'seq')
- image_loss: float32 [8], P('batch')
- text_loss: float32 [8], P('batch')
All inputs are finite; a program needn't handle non-finite values.
Results may differ from a plain program's by a relative error of at most 0.0034.
Values may be sent and summed in bfloat16 or wider, within the bound.
A program may use at most 64 MiB of HBM per device.

v0:
```python
import functools

import jax
import jax.numpy as jnp
from jax import lax
from jax.experimental import pallas as pl
from jax.experimental.pallas import tpu as pltpu
from jax.sharding import PartitionSpec as P

HEADS = 16
HEAD_DIM = 80
EMBED = 1024
LANES = 128
ONES_ROWS = 16
MESH = pl.DeviceIdType.MESH


def fused_kernel(
    nb, nz,
    q_hbm, k_hbm, v_hbm, res_hbm, w_hbm, gain_hbm, wproj_hbm, texts_hbm, labels_hbm,
    hid_hbm, img_ref, txt_ref,
    k_in, q_in, v_in, k_t, q_t, v_t, q_all, k_all, v_all, k_rows,
    gain_ref, texts_ref, labels_ref, o_send, att_t, w_v, res_v, acc, hid_v, wproj_v, text_all, pool_all, row_all,
    in_sem, load_sem, move_send, move_recv, o_ssem, o_rsem,
    text_ssem, text_rsem, wide_ssem, wide_rsem, pool_ssem, pool_rsem, row_ssem, row_rsem, hid_sem,
):
    b = lax.axis_index("batch")
    z = lax.axis_index("seq")
    tok, features = q_in.shape
    local = HEADS // nz
    cols = texts_ref.shape[1]
    half = max(1, nz // 2)
    ends = [-(-(j + 1) * nz * HEAD_DIM // LANES) * LANES for j in range(local)]
    groups = list(zip([0] + ends[:-1], ends))

    def partner(t):
        side = lax.rem(z // half + (1 if t < nz - half else 0), nz // half)
        return side * half + lax.rem(z + t + 1, half)

    barrier = pltpu.get_barrier_semaphore()
    sources, held, turned = (k_hbm, q_hbm, v_hbm), (k_in, q_in, v_in), (k_t, q_t, v_t)

    def in_copy(arr, j):
        at = pl.ds(groups[j][0], groups[j][1] - groups[j][0])
        return pltpu.make_async_copy(
            sources[arr].at[0, :, at], held[arr].at[:, at], in_sem.at[arr, j]
        )

    for t in range(nz - 1):
        pl.semaphore_signal(
            barrier, inc=1, device_id={"seq": partner(t)}, device_id_type=MESH
        )
    for j in range(local):
        for arr in range(3):
            in_copy(arr, j).start()
    for r in range(1, nb):
        pl.semaphore_signal(
            barrier, inc=1, device_id={"batch": lax.rem(b + r, nb)}, device_id_type=MESH
        )
    loads = [
        pltpu.make_async_copy(src, dst, load_sem.at[i])
        for i, (src, dst) in enumerate(
            (
                (res_hbm.at[0], res_v), (wproj_hbm, wproj_v), (w_hbm, w_v),
                (gain_hbm, gain_ref), (labels_hbm, labels_ref),
            )
        )
    ]
    text_load = pltpu.make_async_copy(texts_hbm, texts_ref, load_sem.at[5])
    text_load.start()
    for copy in loads:
        copy.start()

    v_all[:, :, pl.ds(HEAD_DIM, ONES_ROWS), :] = jnp.ones(
        (local, nz, ONES_ROWS, tok), jnp.bfloat16
    )

    def turn(arr, j):
        in_copy(arr, j).wait()
        for at in range(groups[j][0], groups[j][1], LANES):
            turned[arr][pl.ds(at, LANES), :] = held[arr][:, pl.ds(at, LANES)].T

    def piece(arr, j, src):
        return (k_all, q_all, v_all)[arr].at[j, src, pl.ds(0, HEAD_DIM), :]

    def rows_of(arr, j, dst):
        at = pl.multiple_of((j * nz + dst) * HEAD_DIM, 16)
        return turned[arr].at[pl.ds(at, HEAD_DIM), :]

    def remote(arr, j, t):
        dst = partner(t)
        return pltpu.make_async_remote_copy(
            src_ref=rows_of(arr, j, dst),
            dst_ref=piece(arr, j, z),
            send_sem=move_send.at[arr, j, t],
            recv_sem=move_recv.at[arr, j, z],
            device_id={"seq": dst},
            device_id_type=MESH,
        )

    def send_piece(arr, j):
        for t in range(nz - 1):
            remote(arr, j, t).start()
        pltpu.make_async_copy(rows_of(arr, j, z), piece(arr, j, z), move_recv.at[arr, j, z]).start()

    def text_copy(r):
        other = lax.rem(b + r, nb)
        return pltpu.make_async_remote_copy(
            src_ref=texts_ref,
            dst_ref=text_all.at[z, b],
            send_sem=text_ssem.at[r],
            recv_sem=text_rsem.at[b],
            device_id={"batch": other},
            device_id_type=MESH,
        )

    for j in range(local):
        for arr in range(3):
            turn(arr, j)
            if j == arr == 0:
                pl.semaphore_wait(barrier, nz - 1 + nb - 1)
            send_piece(arr, j)
    text_load.wait()
    for r in range(1, nb):
        text_copy(r).start()
    text_all[z, b] = texts_ref[...]

    row_block = min(128, tok)
    chunks = tok // row_block

    def o_rows(j, src, c):
        at = pl.multiple_of(src * HEAD_DIM, 16)
        return att_t.at[j, pl.ds(at, HEAD_DIM), pl.ds(c * row_block, row_block)]

    def o_copy(j, t, c):
        dst = partner(t)
        return pltpu.make_async_remote_copy(
            src_ref=o_send.at[j, dst, :, pl.ds(c * row_block, row_block)],
            dst_ref=o_rows(j, z, c),
            send_sem=o_ssem.at[j, t, c],
            recv_sem=o_rsem.at[j, z, c],
            device_id={"seq": dst},
            device_id_type=MESH,
        )

    def o_arrive(j, c):
        for t in range(nz - 1):
            src = partner(t)
            ref = o_rows(j, src, c)
            pltpu.make_async_copy(ref, ref, o_rsem.at[j, src, c]).wait()

    scale = HEAD_DIM ** (-0.5) * 1.4426950408889634

    def arrive(arr, j):
        for src in range(nz):
            ref = piece(arr, j, src)
            pltpu.make_async_copy(ref, ref, move_recv.at[arr, j, src]).wait()

    def partner_at(t):
        crossing = jnp.where(t < nz - half, 1, 0)
        side = lax.rem(z // half + crossing, nz // half)
        return side * half + lax.rem(z + t + 1, half)

    def attend(index, carry):
        j = index // nz
        t = lax.rem(index, nz)

        @pl.when(t == 0)
        def _():
            arrive(0, j)
            for src in range(nz):
                k_rows[pl.ds(src * tok, tok), :] = k_all[j, src].T
            arrive(1, j)

        dst = partner_at(t)
        s = jnp.dot(k_rows[...], q_all[j, dst], preferred_element_type=jnp.float32)
        p = jnp.exp2((s - jnp.max(s, axis=0, keepdims=True)) * scale).astype(jnp.bfloat16)

        @pl.when(t == 0)
        def _():
            arrive(2, j)

        out = jnp.zeros((HEAD_DIM + ONES_ROWS, tok), jnp.float32)
        for src in range(nz):
            out += jnp.dot(
                v_all[j, src], p[src * tok:(src + 1) * tok], preferred_element_type=jnp.float32
            )
        mixed = (out[:HEAD_DIM] / out[HEAD_DIM:HEAD_DIM + 1]).astype(jnp.bfloat16)

        for at in range(nz - 1):

            @pl.when(t == at)
            def _():
                o_send[j, partner(at)] = mixed
                for c in range(chunks):
                    o_copy(j, at, c).start()

        @pl.when(t == nz - 1)
        def _():
            att_t[j, pl.ds(pl.multiple_of(z * HEAD_DIM, 16), HEAD_DIM), :] = mixed

        return carry

    lax.fori_loop(0, local * nz, attend, 0)

    for copy in loads:
        copy.wait()
    for r in range(1, nb):
        src = lax.rem(b + r, nb)
        ref = text_all.at[z, src]
        pltpu.make_async_copy(ref, ref, text_rsem.at[src]).wait()

    def wide_copy(t):
        return pltpu.make_async_remote_copy(
            src_ref=text_all.at[z],
            dst_ref=text_all.at[z],
            send_sem=wide_ssem.at[t],
            recv_sem=wide_rsem.at[z],
            device_id={"seq": partner(t)},
            device_id_type=MESH,
        )

    for t in range(nz - 1):
        wide_copy(t).start()

    depth = nz * HEAD_DIM

    def product(j, c):
        return jnp.dot(
            att_t[j, :, pl.ds(c * row_block, row_block)].T,
            w_v[pl.ds(j * depth, depth), :],
            preferred_element_type=jnp.float32,
        )

    for j in range(local - 1):
        for c in range(chunks):
            here = pl.ds(c * row_block, row_block)
            o_arrive(j, c)
            old = res_v[here, :].astype(jnp.float32) if j == 0 else acc[here, :]
            acc[here, :] = old + product(j, c)
    for t in range(nz - 1):
        src = partner(t)
        pltpu.make_async_copy(text_all.at[src], text_all.at[src], wide_rsem.at[src]).wait()

    pool = jnp.zeros((1, features), jnp.float32)
    for c in range(chunks):
        here = pl.ds(c * row_block, row_block)
        o_arrive(local - 1, c)
        old = res_v[here, :].astype(jnp.float32) if local == 1 else acc[here, :]
        summed = old + product(local - 1, c)
        hid_v[here, :] = summed.astype(jnp.bfloat16)
        pltpu.make_async_copy(hid_v.at[here, :], hid_hbm.at[0, here, :], hid_sem.at[c]).start()
        centred = summed - jnp.mean(summed, axis=-1, keepdims=True)
        variance = jnp.mean(centred * centred, axis=-1, keepdims=True)
        pool += jnp.sum(centred * lax.rsqrt(variance + 1e-05), axis=0, keepdims=True)

    pool_all[z] = pool * gain_ref[...].reshape(1, features)

    def pool_copy(t):
        return pltpu.make_async_remote_copy(
            src_ref=pool_all.at[z],
            dst_ref=pool_all.at[z],
            send_sem=pool_ssem.at[t],
            recv_sem=pool_rsem.at[z],
            device_id={"seq": partner(t)},
            device_id_type=MESH,
        )

    for t in range(nz - 1):
        pool_copy(t).start()
    for t in range(nz - 1):
        src = partner(t)
        pltpu.make_async_copy(pool_all.at[src], pool_all.at[src], pool_rsem.at[src]).wait()
    pooled = pool_all[0]
    for src in range(1, nz):
        pooled = pooled + pool_all[src]
    pooled = pooled / (nz * tok)

    high = pooled.astype(jnp.bfloat16).astype(jnp.float32)
    middle = (pooled - high).astype(jnp.bfloat16).astype(jnp.float32)
    low = pooled - high - middle
    row_id = lax.broadcasted_iota(jnp.int32, (16, features), 0)
    parts = jnp.where(
        row_id == 0, high, jnp.where(row_id == 1, middle, jnp.where(row_id == 2, low, 0.0))
    ).astype(jnp.bfloat16)
    embed = jnp.sum(
        jnp.dot(parts, wproj_v[...], preferred_element_type=jnp.float32), axis=0, keepdims=True
    )
    products = jnp.zeros((nb, 1), jnp.float32)
    for src in range(nz):
        texts = text_all[src].reshape(nb, cols)
        products += jnp.sum(
            texts * embed[:, src * cols:(src + 1) * cols], axis=1, keepdims=True
        )
    squares = jnp.sum(embed * embed, axis=1, keepdims=True)
    rows = lax.broadcasted_iota(jnp.int32, (nb, LANES), 0)
    lanes = lax.broadcasted_iota(jnp.int32, (nb, LANES), 1)
    row = jnp.sum(jnp.where(rows == lanes, products, 0.0), axis=0, keepdims=True)
    row_all[b] = jnp.where(lanes[:1] == nb, squares, row)

    def row_copy(r):
        return pltpu.make_async_remote_copy(
            src_ref=row_all.at[b],
            dst_ref=row_all.at[b],
            send_sem=row_ssem.at[r],
            recv_sem=row_rsem.at[b],
            device_id={"batch": lax.rem(b + r, nb)},
            device_id_type=MESH,
        )

    for r in range(1, nb):
        row_copy(r).start()

    for t in range(nz - 1):
        for j in range(local):
            for arr in range(3):
                remote(arr, j, t).wait_send()
            for c in range(chunks):
                o_copy(j, t, c).wait_send()
        pool_copy(t).wait_send()
        wide_copy(t).wait_send()
    for c in range(chunks):
        here = pl.ds(c * row_block, row_block)
        pltpu.make_async_copy(hid_v.at[here, :], hid_hbm.at[0, here, :], hid_sem.at[c]).wait()
    for r in range(1, nb):
        text_copy(r).wait_send()

    for r in range(1, nb):
        src = lax.rem(b + r, nb)
        pltpu.make_async_copy(row_all.at[src], row_all.at[src], row_rsem.at[src]).wait()
    total = row_all[...].reshape(nb, LANES)
    norm = jnp.sum(jnp.where(lanes == nb, total, 0.0), axis=1, keepdims=True)
    logits = total * lax.rsqrt(norm + 1e-06)
    valid = lanes < nb
    matching = jnp.zeros((nb, LANES), jnp.int32)
    for i in range(nb):
        matching = jnp.where(rows == i, labels_ref[i], matching)
    picked = jnp.where(matching == lanes, logits, 0.0)
    shown = jnp.where(valid, logits, -3e38)
    top = jnp.max(shown, axis=1, keepdims=True)
    image = (
        top
        + jnp.log(jnp.sum(jnp.where(valid, jnp.exp(shown - top), 0.0), axis=1, keepdims=True))
        - jnp.sum(jnp.where(valid, picked, 0.0), axis=1, keepdims=True)
    )
    peak = jnp.max(logits, axis=0, keepdims=True)
    text = (
        peak
        + jnp.log(jnp.sum(jnp.exp(logits - peak), axis=0, keepdims=True))
        - jnp.sum(picked, axis=0, keepdims=True)
    )
    img_ref[0] = jnp.sum(jnp.where((rows == b) & (lanes == 0), image, 0.0))
    txt_ref[0] = jnp.sum(jnp.where((rows == 0) & (lanes == b), text, 0.0))
    for r in range(1, nb):
        row_copy(r).wait_send()


def fused(queries, keys, values, residual_in, w_out, ln_gain, w_proj, texts, labels):
    nb, nz = lax.axis_size("batch"), lax.axis_size("seq")
    _, tok, features = queries.shape
    local = HEADS // nz
    chunks = tok // min(128, tok)
    cols = texts.shape[1]
    bf16, f32 = jnp.bfloat16, jnp.float32
    anywhere = pl.BlockSpec(memory_space=pl.ANY)
    smem = pl.BlockSpec(memory_space=pltpu.SMEM)
    dma = pltpu.SemaphoreType.DMA
    wide = pltpu.VMEM((tok, features), bf16)
    tall = pltpu.VMEM((features, tok), bf16)
    return pl.pallas_call(
        functools.partial(fused_kernel, nb, nz),
        out_shape=(
            jax.ShapeDtypeStruct((1, tok, features), bf16),
            jax.ShapeDtypeStruct((1,), f32),
            jax.ShapeDtypeStruct((1,), f32),
        ),
        in_specs=[pl.BlockSpec(memory_space=pltpu.HBM)] * 9,
        out_specs=(anywhere, smem, smem),
        scratch_shapes=[
            wide, wide, wide, tall, tall, tall,
            pltpu.VMEM((local, nz, HEAD_DIM, tok), bf16),
            pltpu.VMEM((local, nz, HEAD_DIM, tok), bf16),
            pltpu.VMEM((local, nz, HEAD_DIM + ONES_ROWS, tok), bf16),
            pltpu.VMEM((nz * tok, HEAD_DIM), bf16),
            pltpu.VMEM((features,), f32),
            pltpu.VMEM((1, cols), f32),
            pltpu.SMEM(labels.shape, jnp.int32),
            pltpu.VMEM((local, nz, HEAD_DIM, tok), bf16),
            pltpu.VMEM((local, nz * HEAD_DIM, tok), bf16),
            pltpu.VMEM((features, features), bf16),
            wide,
            pltpu.VMEM((tok, features), f32),
            wide,
            pltpu.VMEM(w_proj.shape, bf16),
            pltpu.VMEM((nz, nb, 1, cols), f32),
            pltpu.VMEM((nz, 1, features), f32),
            pltpu.VMEM((nb, 1, LANES), f32),
            dma((3, local)), dma((6,)),
            dma((3, local, nz)), dma((3, local, nz)),
            dma((local, nz, chunks)), dma((local, nz, chunks)),
            dma((nb,)), dma((nb,)), dma((nz,)), dma((nz,)), dma((nz,)), dma((nz,)),
            dma((nb,)), dma((nb,)), dma((chunks,)),
        ],
        compiler_params=pltpu.CompilerParams(
            collective_id=0, has_side_effects=True, vmem_limit_bytes=40 * 1024 * 1024
        ),
    )(
        *(pltpu.with_memory_space_constraint(x, pltpu.HBM) for x in (queries, keys, values, residual_in, w_out, ln_gain, w_proj,
        texts, labels))
    )


def row_lse(logits, axis):
    maxima = jnp.max(logits, axis=axis, keepdims=True)
    return jnp.squeeze(maxima, axis) + jnp.log(jnp.sum(jnp.exp(logits - maxima), axis=axis))


def body(queries, keys, values, residual_in, w_out, ln_gain, w_proj, texts, labels):
    seq_count = lax.axis_size("seq")
    images_here, tok_rows, features = queries.shape
    head_count = HEADS // seq_count
    head_cols = head_count * HEAD_DIM
    score_scale = HEAD_DIM ** (-0.5)
    query_all = lax.all_to_all(queries, "seq", split_axis=2, concat_axis=1, tiled=True)
    key_all = lax.all_to_all(keys, "seq", split_axis=2, concat_axis=1, tiled=True)
    value_all = lax.all_to_all(values, "seq", split_axis=2, concat_axis=1, tiled=True)
    items = query_all.shape[0]
    length = query_all.shape[1]
    block_rows = min(512, length)
    query_heads = query_all.reshape(items, length, head_count, HEAD_DIM)
    key_heads = key_all.reshape(items, length, head_count, HEAD_DIM)
    value_heads = value_all.reshape(items, length, head_count, HEAD_DIM)

    def one_block(offset):
        query_block = lax.dynamic_slice_in_dim(query_heads, offset, block_rows, 1)
        scores = (
            jnp.einsum(
                "nqhd,nkhd->nhqk", query_block, key_heads, preferred_element_type=jnp.float32
            )
            * score_scale
        )
        maxima = jnp.max(scores, axis=-1, keepdims=True)
        weights = jnp.exp(scores - maxima)
        weights = (weights / jnp.sum(weights, axis=-1, keepdims=True)).astype(jnp.bfloat16)
        mixed = jnp.einsum(
            "nhqk,nkhd->nqhd", weights, value_heads, preferred_element_type=jnp.float32
        )
        return mixed.astype(jnp.bfloat16).reshape(items, block_rows, head_cols)

    offsets = jnp.arange(length // block_rows) * block_rows
    blocks = lax.map(one_block, offsets)
    attended = jnp.moveaxis(blocks, 0, 1).reshape(items, length, head_cols)
    attended = lax.all_to_all(attended, "seq", split_axis=1, concat_axis=2, tiled=True)
    mixed_out = jnp.dot(attended.reshape(-1, features), w_out, preferred_element_type=jnp.float32)
    summed = residual_in.astype(jnp.float32) + mixed_out.reshape(images_here, tok_rows, features)
    hidden_out = summed.astype(jnp.bfloat16)
    centred = summed - jnp.mean(summed, axis=-1, keepdims=True)
    variance = jnp.mean(centred * centred, axis=-1, keepdims=True)
    normed = centred * lax.rsqrt(variance + 1e-05) * ln_gain
    pool_part = jnp.sum(normed, axis=1) / (tok_rows * seq_count)
    embed_cols = EMBED // seq_count
    pooled = lax.psum(pool_part, "seq")
    embedding = jnp.dot(pooled, w_proj.astype(jnp.float32), precision=lax.Precision.HIGHEST)
    inverse = lax.rsqrt(jnp.sum(embedding * embedding, axis=1) + 1e-06)
    unit_rows = embedding * inverse[:, None]
    embed_piece = lax.dynamic_slice_in_dim(
        unit_rows, lax.axis_index("seq") * embed_cols, embed_cols, 1
    )
    gathered, text_all = (
        lax.all_gather(embed_piece, "batch", axis=0, tiled=True),
        lax.all_gather(texts, "batch", axis=0, tiled=True),
    )
    logit_part = jnp.dot(gathered, text_all.T, precision=lax.Precision.HIGHEST)
    logits = lax.psum(logit_part, "seq")
    matched = labels[:, None] == jnp.arange(logits.shape[1], dtype=jnp.int32)[None, :]
    picked = jnp.where(matched, logits, jnp.float32(0.0))
    image_all = row_lse(logits, 1) - jnp.sum(picked, axis=1)
    text_every = row_lse(logits, 0) - jnp.sum(picked, axis=0)
    first_row = lax.axis_index("batch") * images_here
    image_loss = lax.dynamic_slice_in_dim(image_all, first_row, images_here, 0)
    text_loss = lax.dynamic_slice_in_dim(text_every, first_row, images_here, 0)
    return (hidden_out, image_loss, text_loss)


def program(queries, keys, values, residual_in, w_out, ln_gain, w_proj, texts, labels):
    nb, nz = lax.axis_size("batch"), lax.axis_size("seq")
    fits = (
        queries.shape[0] == 1
        and texts.shape[0] == 1
        and HEADS % nz == 0
        and nz % 2 == 0
        and HEADS * HEAD_DIM % LANES == 0
        and queries.shape[1] % 128 == 0
        and queries.shape[1] <= 512
        and queries.shape[1] * nz <= 2048
        and texts.shape[1] % LANES == 0
        and nb % 8 == 0
        and nb < LANES
    )
    chosen = fused if fits else body
    return chosen(queries, keys, values, residual_in, w_out, ln_gain, w_proj, texts, labels)


def solution(mesh):
    in_specs = (
        P("batch", "seq", None),
        P("batch", "seq", None),
        P("batch", "seq", None),
        P("batch", "seq", None),
        P(),
        P(),
        P(),
        P("batch", "seq"),
        P(),
    )
    out_specs = (P("batch", "seq", None), P("batch"), P("batch"))
    return jax.shard_map(program, mesh=mesh, in_specs=in_specs, out_specs=out_specs, check_vma=False)
```

profile of v0, /device:TPU:0, one launch (start us, length us, event | category | flops | bytes accessed | tf_op | source)
XLA Modules:
  0.0 139.5 jit_solution(6865908701575562407)
XLA Ops:
  0.6 134.4 %shard_map.112 = (bf16[1,512,1280]{2,1,0:T(8,128)(2,1)S(1)}, f32[1]{0:T(128)}, f32[1]{0:T(128)}) custom-call(bf16[1,512,1280]{2,1,0:T(8,128)(2,1)} %q_hbm.1, bf16[1,512,1280]{2,1,0:T(8,128)(2,1)} %k_hbm.1, bf16[1,512,1280]{2,1,0:T(8,128)(2,1)} %v_hbm.1, bf16[1,512,1280]{2,1,0:T(8,128)(2,1)} %res_hbm.1, bf16[1280,1280]{1,0:T(8,128)(2,1)} %w_hbm.1, ...), custom_call_target="tpu_custom_call" | custom-call | tf_op jit(solution)/shard_map/pallas_call | solution.py:370
  135.0 1.1 copy.15
where the time goes:
time: 140 us
  Pallas kernels  134 us (96%)
  between operations  4.09 us (3%)
    pallas_call x1, Pallas kernels, fused(): pl.pallas_call(functools.partial(fused_kernel, nb, nz), out_shape=(jax.Sh...  134 us

commit v1 on v0

--- a/solution.py
+++ b/solution.py
@@ -17,10 +17,10 @@
 
 def fused_kernel(
     nb, nz,
-    q_hbm, k_hbm, v_hbm, res_hbm, w_hbm, gain_hbm, wproj_hbm, texts_hbm, labels_hbm,
-    hid_hbm, img_ref, txt_ref,
+    q_hbm, k_hbm, v_hbm, res_hbm, w_hbm, gain_hbm, wproj_hbm, texts_hbm,
+    hid_out, row_out,
     k_in, q_in, v_in, k_t, q_t, v_t, q_all, k_all, v_all, k_rows,
-    gain_ref, texts_ref, labels_ref, o_send, att_t, w_v, res_v, acc, hid_v, wproj_v, text_all, pool_all, row_all,
+    gain_ref, texts_ref, o_send, att_t, w_v, res_v, acc, hid_v, wproj_v, text_all, pool_all, row_all,
     in_sem, load_sem, move_send, move_recv, o_ssem, o_rsem,
     text_ssem, text_rsem, wide_ssem, wide_rsem, pool_ssem, pool_rsem, row_ssem, row_rsem, hid_sem,
 ):
@@ -62,11 +62,11 @@
         for i, (src, dst) in enumerate(
             (
                 (res_hbm.at[0], res_v), (wproj_hbm, wproj_v), (w_hbm, w_v),
-                (gain_hbm, gain_ref), (labels_hbm, labels_ref),
+                (gain_hbm, gain_ref),
             )
         )
     ]
-    text_load = pltpu.make_async_copy(texts_hbm, texts_ref, load_sem.at[5])
+    text_load = pltpu.make_async_copy(texts_hbm, texts_ref, load_sem.at[4])
     text_load.start()
     for copy in loads:
         copy.start()
@@ -92,8 +92,8 @@
         return pltpu.make_async_remote_copy(
             src_ref=rows_of(arr, j, dst),
             dst_ref=piece(arr, j, z),
-            send_sem=move_send.at[arr, j, t],
-            recv_sem=move_recv.at[arr, j, z],
+            send_sem=move_send.at[arr],
+            recv_sem=move_recv.at[arr, j],
             device_id={"seq": dst},
             device_id_type=MESH,
         )
@@ -101,18 +101,30 @@
     def send_piece(arr, j):
         for t in range(nz - 1):
             remote(arr, j, t).start()
-        pltpu.make_async_copy(rows_of(arr, j, z), piece(arr, j, z), move_recv.at[arr, j, z]).start()
-
-    def text_copy(r):
-        other = lax.rem(b + r, nb)
+        pltpu.make_async_copy(rows_of(arr, j, z), piece(arr, j, z), move_recv.at[arr, j]).start()
+
+    def text_copy(t):
         return pltpu.make_async_remote_copy(
             src_ref=texts_ref,
-            dst_ref=text_all.at[z, b],
-            send_sem=text_ssem.at[r],
-            recv_sem=text_rsem.at[b],
-            device_id={"batch": other},
+            dst_ref=text_all.at[b, z],
+            send_sem=text_ssem,
+            recv_sem=text_rsem,
+            device_id={"seq": partner(t)},
             device_id_type=MESH,
         )
+
+    def wide_copy(r):
+        return pltpu.make_async_remote_copy(
+            src_ref=text_all.at[b],
+            dst_ref=text_all.at[b],
+            send_sem=wide_ssem,
+            recv_sem=wide_rsem,
+            device_id={"batch": lax.rem(b + r, nb)},
+            device_id_type=MESH,
+        )
+
+    def await_bytes(ref, sem):
+        pltpu.make_async_copy(ref, ref, sem).wait()
 
     for j in range(local):
         for arr in range(3):
@@ -120,10 +132,11 @@
             if j == arr == 0:
                 pl.semaphore_wait(barrier, nz - 1 + nb - 1)
             send_piece(arr, j)
-    text_load.wait()
-    for r in range(1, nb):
-        text_copy(r).start()
-    text_all[z, b] = texts_ref[...]
+            if j == arr == 0:
+                text_load.wait()
+                for t in range(nz - 1):
+                    text_copy(t).start()
+                text_all[b, z] = texts_ref[...]
 
     row_block = min(128, tok)
     chunks = tok // row_block
@@ -137,24 +150,22 @@
         return pltpu.make_async_remote_copy(
             src_ref=o_send.at[j, dst, :, pl.ds(c * row_block, row_block)],
             dst_ref=o_rows(j, z, c),
-            send_sem=o_ssem.at[j, t, c],
-            recv_sem=o_rsem.at[j, z, c],
+            send_sem=o_ssem,
+            recv_sem=o_rsem.at[j, c],
             device_id={"seq": dst},
             device_id_type=MESH,
         )
 
     def o_arrive(j, c):
-        for t in range(nz - 1):
-            src = partner(t)
-            ref = o_rows(j, src, c)
-            pltpu.make_async_copy(ref, ref, o_rsem.at[j, src, c]).wait()
-
+        here = pl.ds(c * row_block, row_block)
+        await_bytes(att_t.at[j, pl.ds(0, (nz - 1) * HEAD_DIM), here], o_rsem.at[j, c])
+
+    far = nz - half
     scale = HEAD_DIM ** (-0.5) * 1.4426950408889634
 
     def arrive(arr, j):
-        for src in range(nz):
-            ref = piece(arr, j, src)
-            pltpu.make_async_copy(ref, ref, move_recv.at[arr, j, src]).wait()
+        ref = (k_all, q_all, v_all)[arr].at[j, :, pl.ds(0, HEAD_DIM), :]
+        await_bytes(ref, move_recv.at[arr, j])
 
     def partner_at(t):
         crossing = jnp.where(t < nz - half, 1, 0)
@@ -192,37 +203,36 @@
             @pl.when(t == at)
             def _():
                 o_send[j, partner(at)] = mixed
-                for c in range(chunks):
-                    o_copy(j, at, c).start()
+
+                @pl.when((j < local - 1) | (at >= far))
+                def _():
+                    for c in range(chunks):
+                        o_copy(j, at, c).start()
+
+                if at == far - 1:
+
+                    @pl.when(j == local - 1)
+                    def _():
+                        for c in range(chunks):
+                            for near in range(far):
+                                o_copy(j, near, c).start()
 
         @pl.when(t == nz - 1)
         def _():
             att_t[j, pl.ds(pl.multiple_of(z * HEAD_DIM, 16), HEAD_DIM), :] = mixed
 
+        @pl.when((j == 0) & (t == nz - 1))
+        def _():
+            await_bytes(text_all.at[b, pl.ds(0, nz - 1)], text_rsem)
+            for r in range(1, nb):
+                wide_copy(r).start()
+
         return carry
 
     lax.fori_loop(0, local * nz, attend, 0)
 
     for copy in loads:
         copy.wait()
-    for r in range(1, nb):
-        src = lax.rem(b + r, nb)
-        ref = text_all.at[z, src]
-        pltpu.make_async_copy(ref, ref, text_rsem.at[src]).wait()
-
-    def wide_copy(t):
-        return pltpu.make_async_remote_copy(
-            src_ref=text_all.at[z],
-            dst_ref=text_all.at[z],
-            send_sem=wide_ssem.at[t],
-            recv_sem=wide_rsem.at[z],
-            device_id={"seq": partner(t)},
-            device_id_type=MESH,
-        )
-
-    for t in range(nz - 1):
-        wide_copy(t).start()
-
     depth = nz * HEAD_DIM
 
     def product(j, c):
@@ -238,9 +248,7 @@
             o_arrive(j, c)
             old = res_v[here, :].astype(jnp.float32) if j == 0 else acc[here, :]
             acc[here, :] = old + product(j, c)
-    for t in range(nz - 1):
-        src = partner(t)
-        pltpu.make_async_copy(text_all.at[src], text_all.at[src], wide_rsem.at[src]).wait()
+    await_bytes(text_all.at[pl.ds(0, nb - 1)], wide_rsem)
 
     pool = jnp.zeros((1, features), jnp.float32)
     for c in range(chunks):
@@ -249,7 +257,7 @@
         old = res_v[here, :].astype(jnp.float32) if local == 1 else acc[here, :]
         summed = old + product(local - 1, c)
         hid_v[here, :] = summed.astype(jnp.bfloat16)
-        pltpu.make_async_copy(hid_v.at[here, :], hid_hbm.at[0, here, :], hid_sem.at[c]).start()
+        pltpu.make_async_copy(hid_v.at[here, :], hid_out.at[0, here, :], hid_sem).start()
         centred = summed - jnp.mean(summed, axis=-1, keepdims=True)
         variance = jnp.mean(centred * centred, axis=-1, keepdims=True)
         pool += jnp.sum(centred * lax.rsqrt(variance + 1e-05), axis=0, keepdims=True)
@@ -260,17 +268,15 @@
         return pltpu.make_async_remote_copy(
             src_ref=pool_all.at[z],
             dst_ref=pool_all.at[z],
-            send_sem=pool_ssem.at[t],
-            recv_sem=pool_rsem.at[z],
+            send_sem=pool_ssem,
+            recv_sem=pool_rsem,
             device_id={"seq": partner(t)},
             device_id_type=MESH,
         )
 
     for t in range(nz - 1):
         pool_copy(t).start()
-    for t in range(nz - 1):
-        src = partner(t)
-        pltpu.make_async_copy(pool_all.at[src], pool_all.at[src], pool_rsem.at[src]).wait()
+    await_bytes(pool_all.at[pl.ds(0, nz - 1)], pool_rsem)
     pooled = pool_all[0]
     for src in range(1, nz):
         pooled = pooled + pool_all[src]
@@ -288,7 +294,7 @@
     )
     products = jnp.zeros((nb, 1), jnp.float32)
     for src in range(nz):
-        texts = text_all[src].reshape(nb, cols)
+        texts = text_all[:, src].reshape(nb, cols)
         products += jnp.sum(
             texts * embed[:, src * cols:(src + 1) * cols], axis=1, keepdims=True
         )
@@ -302,8 +308,8 @@
         return pltpu.make_async_remote_copy(
             src_ref=row_all.at[b],
             dst_ref=row_all.at[b],
-            send_sem=row_ssem.at[r],
-            recv_sem=row_rsem.at[b],
+            send_sem=row_ssem,
+            recv_sem=row_rsem,
             device_id={"batch": lax.rem(b + r, nb)},
             device_id_type=MESH,
         )
@@ -311,24 +317,25 @@
     for r in range(1, nb):
         row_copy(r).start()
 
-    for t in range(nz - 1):
-        for j in range(local):
-            for arr in range(3):
-                remote(arr, j, t).wait_send()
-            for c in range(chunks):
-                o_copy(j, t, c).wait_send()
-        pool_copy(t).wait_send()
-        wide_copy(t).wait_send()
-    for c in range(chunks):
-        here = pl.ds(c * row_block, row_block)
-        pltpu.make_async_copy(hid_v.at[here, :], hid_hbm.at[0, here, :], hid_sem.at[c]).wait()
-    for r in range(1, nb):
-        text_copy(r).wait_send()
-
-    for r in range(1, nb):
-        src = lax.rem(b + r, nb)
-        pltpu.make_async_copy(row_all.at[src], row_all.at[src], row_rsem.at[src]).wait()
-    total = row_all[...].reshape(nb, LANES)
+    for arr in range(3):
+        await_bytes(k_all.at[:, pl.ds(0, nz - 1)], move_send.at[arr])
+    await_bytes(o_send.at[:, pl.ds(0, nz - 1)], o_ssem)
+    await_bytes(text_all.at[b, pl.ds(0, nz - 1)], text_ssem)
+    await_bytes(text_all.at[pl.ds(0, nb - 1)], wide_ssem)
+    await_bytes(pool_all.at[pl.ds(0, nz - 1)], pool_ssem)
+    pltpu.make_async_copy(hid_v, hid_out.at[0], hid_sem).wait()
+    await_bytes(row_all.at[pl.ds(0, nb - 1)], row_rsem)
+    row_out[...] = row_all[...].reshape(nb, LANES)
+    await_bytes(row_all.at[pl.ds(0, nb - 1)], row_ssem)
+
+
+def loss_kernel(nb, hid_ref, row_ref, labels_ref, hid_out, img_ref, txt_ref, sem):
+    store = pltpu.make_async_copy(hid_ref, hid_out, sem)
+    store.start()
+    b = lax.axis_index("batch")
+    rows = lax.broadcasted_iota(jnp.int32, (nb, LANES), 0)
+    lanes = lax.broadcasted_iota(jnp.int32, (nb, LANES), 1)
+    total = row_ref[...]
     norm = jnp.sum(jnp.where(lanes == nb, total, 0.0), axis=1, keepdims=True)
     logits = total * lax.rsqrt(norm + 1e-06)
     valid = lanes < nb
@@ -351,8 +358,7 @@
     )
     img_ref[0] = jnp.sum(jnp.where((rows == b) & (lanes == 0), image, 0.0))
     txt_ref[0] = jnp.sum(jnp.where((rows == 0) & (lanes == b), text, 0.0))
-    for r in range(1, nb):
-        row_copy(r).wait_send()
+    store.wait()
 
 
 def fused(queries, keys, values, residual_in, w_out, ln_gain, w_proj, texts, labels):
@@ -367,15 +373,12 @@
     dma = pltpu.SemaphoreType.DMA
     wide = pltpu.VMEM((tok, features), bf16)
     tall = pltpu.VMEM((features, tok), bf16)
-    return pl.pallas_call(
+    hidden_shape = jax.ShapeDtypeStruct((1, tok, features), bf16)
+    hidden, rows = pl.pallas_call(
         functools.partial(fused_kernel, nb, nz),
-        out_shape=(
-            jax.ShapeDtypeStruct((1, tok, features), bf16),
-            jax.ShapeDtypeStruct((1,), f32),
-            jax.ShapeDtypeStruct((1,), f32),
-        ),
-        in_specs=[pl.BlockSpec(memory_space=pltpu.HBM)] * 9,
-        out_specs=(anywhere, smem, smem),
+        out_shape=(hidden_shape, jax.ShapeDtypeStruct((nb, LANES), f32)),
+        in_specs=[pl.BlockSpec(memory_space=pltpu.HBM)] * 8,
+        out_specs=(anywhere, pl.BlockSpec(memory_space=pltpu.VMEM)),
         scratch_shapes=[
             wide, wide, wide, tall, tall, tall,
             pltpu.VMEM((local, nz, HEAD_DIM, tok), bf16),
@@ -384,7 +387,6 @@
             pltpu.VMEM((nz * tok, HEAD_DIM), bf16),
             pltpu.VMEM((features,), f32),
             pltpu.VMEM((1, cols), f32),
-            pltpu.SMEM(labels.shape, jnp.int32),
             pltpu.VMEM((local, nz, HEAD_DIM, tok), bf16),
             pltpu.VMEM((local, nz * HEAD_DIM, tok), bf16),
             pltpu.VMEM((features, features), bf16),
@@ -392,22 +394,31 @@
             pltpu.VMEM((tok, features), f32),
             wide,
             pltpu.VMEM(w_proj.shape, bf16),
-            pltpu.VMEM((nz, nb, 1, cols), f32),
+            pltpu.VMEM((nb, nz, 1, cols), f32),
             pltpu.VMEM((nz, 1, features), f32),
             pltpu.VMEM((nb, 1, LANES), f32),
-            dma((3, local)), dma((6,)),
-            dma((3, local, nz)), dma((3, local, nz)),
-            dma((local, nz, chunks)), dma((local, nz, chunks)),
-            dma((nb,)), dma((nb,)), dma((nz,)), dma((nz,)), dma((nz,)), dma((nz,)),
-            dma((nb,)), dma((nb,)), dma((chunks,)),
+            dma((3, local)), dma((5,)),
+            dma((3,)), dma((3, local)),
+            dma, dma((local, chunks)),
+            dma, dma, dma, dma, dma, dma, dma, dma, dma,
         ],
         compiler_params=pltpu.CompilerParams(
             collective_id=0, has_side_effects=True, vmem_limit_bytes=40 * 1024 * 1024
         ),
     )(
         *(pltpu.with_memory_space_constraint(x, pltpu.HBM) for x in (queries, keys, values, residual_in, w_out, ln_gain, w_proj,
-        texts, labels))
-    )
+        texts))
+    )
+    return pl.pallas_call(
+        functools.partial(loss_kernel, nb),
+        out_shape=(
+            hidden_shape, jax.ShapeDtypeStruct((1,), f32), jax.ShapeDtypeStruct((1,), f32),
+        ),
+        in_specs=[anywhere, pl.BlockSpec(memory_space=pltpu.VMEM), smem],
+        out_specs=(pl.BlockSpec(memory_space=pltpu.HBM), smem, smem),
+        scratch_shapes=[dma],
+        compiler_params=pltpu.CompilerParams(vmem_limit_bytes=4 * 1024 * 1024),
+    )(hidden, rows, labels)
 
 
 def row_lse(logits, axis):

time: 140 us -> 132 us (0.943)
  between operations: 4.09 us -> 0.66 us
  Pallas kernels: 134 us -> 131 us
    pallas_call x1 -> x2, Pallas kernels: 134 us -> 131 us  [the longest x1 129 us: fused(): pl.pallas_call(functools.partial(fused_kernel, nb, nz), out_shape=(hidden...]
where the time goes in v1:
time: 132 us
  Pallas kernels  131 us (99%)
    pallas_call x1, Pallas kernels, fused(): pl.pallas_call(functools.partial(fused_kernel, nb, nz), out_shape=(hidden...  129 us

profile of v1, /device:TPU:0, one launch (start us, length us, event | category | flops | bytes accessed | tf_op | source)
XLA Modules:
  0.0 131.9 jit_solution(17451880878107603814)
XLA Ops:
  0.6 0.0 copy-start
  0.6 129.1 %shard_map.112 = (bf16[1,512,1280]{2,1,0:T(8,128)(2,1)S(1)}, f32[8,128]{1,0:T(8,128)S(1)}) custom-call(bf16[1,512,1280]{2,1,0:T(8,128)(2,1)} %q_hbm.1, bf16[1,512,1280]{2,1,0:T(8,128)(2,1)} %k_hbm.1, bf16[1,512,1280]{2,1,0:T(8,128)(2,1)} %v_hbm.1, bf16[1,512,1280]{2,1,0:T(8,128)(2,1)} %res_hbm.1, bf16[1280,1280]{1,0:T(8,128)(2,1)} %w_hbm.1, f32[1280]{0:T(1024)} %gain_hbm.1, ...), custom_call_target="tpu_custom_call" | custom-call | tf_op jit(solution)/shard_map/pallas_call | solution.py:377
  129.7 0.0 copy-done
  129.7 2.1 %shard_map.113 = (bf16[1,512,1280]{2,1,0:T(8,128)(2,1)}, f32[1]{0:T(128)}, f32[1]{0:T(128)}) custom-call(bf16[1,512,1280]{2,1,0:T(8,128)(2,1)S(1)} %get-tuple-element.5.hid_ref, f32[8,128]{1,0:T(8,128)S(1)} %get-tuple-element.6.row_ref, s32[8]{0:T(128)S(1)} %copy-done), custom_call_target="tpu_custom_call" | custom-call | tf_op jit(solution)/shard_map/pallas_call | solution.py:412
Async XLA Ops:
  0.6 129.1 %copy-start = (s32[8]{0:T(128)S(1)}, s32[8]{0:T(128)}, u32[]{:S(2)}) copy-start(s32[8]{0:T(128)} %labels_ref.1) | copy-start | bytes 100

commit v2 on v1

--- a/solution.py
+++ b/solution.py
@@ -17,16 +17,16 @@
 
 def fused_kernel(
     nb, nz,
-    q_hbm, k_hbm, v_hbm, res_hbm, w_hbm, gain_hbm, wproj_hbm, texts_hbm,
-    hid_out, row_out,
-    k_in, q_in, v_in, k_t, q_t, v_t, q_all, k_all, v_all, k_rows,
-    gain_ref, texts_ref, o_send, att_t, w_v, res_v, acc, hid_v, wproj_v, text_all, pool_all, row_all,
-    in_sem, load_sem, move_send, move_recv, o_ssem, o_rsem,
+    q_hbm, k_hbm, v_hbm, res_hbm, w_hbm, gain_hbm, wproj_hbm, texts_hbm, labels_hbm,
+    hid_out, row_out, match_out,
+    inputs, k_t, q_t, v_t, kq_all, v_all, k_rows,
+    gain_ref, texts_ref, labels_ref, o_send, att_t, w_v, res_v, acc, hid_v, wproj_v, text_all, pool_all, row_all,
+    in_sem, load_sem, w_sem, move_send, move_recv, o_ssem, o_rsem,
     text_ssem, text_rsem, wide_ssem, wide_rsem, pool_ssem, pool_rsem, row_ssem, row_rsem, hid_sem,
 ):
     b = lax.axis_index("batch")
     z = lax.axis_index("seq")
-    tok, features = q_in.shape
+    _, tok, features = inputs.shape
     local = HEADS // nz
     cols = texts_ref.shape[1]
     half = max(1, nz // 2)
@@ -38,12 +38,16 @@
         return side * half + lax.rem(z + t + 1, half)
 
     barrier = pltpu.get_barrier_semaphore()
-    sources, held, turned = (k_hbm, q_hbm, v_hbm), (k_in, q_in, v_in), (k_t, q_t, v_t)
+    sources, turned = (k_hbm, q_hbm, v_hbm), (k_t, q_t, v_t)
+
+    def columns(j):
+        return pl.ds(groups[j][0], groups[j][1] - groups[j][0])
 
     def in_copy(arr, j):
-        at = pl.ds(groups[j][0], groups[j][1] - groups[j][0])
         return pltpu.make_async_copy(
-            sources[arr].at[0, :, at], held[arr].at[:, at], in_sem.at[arr, j]
+            sources[arr].at[0, :, columns(j)],
+            inputs.at[arr, :, columns(j)],
+            in_sem.at[arr if j == 0 else 2 + j],
         )
 
     for t in range(nz - 1):
@@ -61,27 +65,51 @@
         pltpu.make_async_copy(src, dst, load_sem.at[i])
         for i, (src, dst) in enumerate(
             (
-                (res_hbm.at[0], res_v), (wproj_hbm, wproj_v), (w_hbm, w_v),
-                (gain_hbm, gain_ref),
+                (res_hbm.at[0], res_v), (wproj_hbm, wproj_v), (gain_hbm, gain_ref),
+                (labels_hbm, labels_ref),
             )
         )
     ]
+    w_rows = []
+    for j in range(local):
+        for at in range(nz):
+            across = lax.rem(at + half, nz)
+            src = jnp.where(z < half, nz - 1 - across, across)
+            start = pl.multiple_of((j * nz + src) * HEAD_DIM, 16)
+            w_rows.append(
+                pltpu.make_async_copy(
+                    w_hbm.at[pl.ds(start, HEAD_DIM)],
+                    w_v.at[pl.ds((j * nz + at) * HEAD_DIM, HEAD_DIM)],
+                    w_sem,
+                )
+            )
     text_load = pltpu.make_async_copy(texts_hbm, texts_ref, load_sem.at[4])
     text_load.start()
-    for copy in loads:
+    for copy in loads + w_rows:
         copy.start()
 
     v_all[:, :, pl.ds(HEAD_DIM, ONES_ROWS), :] = jnp.ones(
         (local, nz, ONES_ROWS, tok), jnp.bfloat16
     )
 
+    def await_bytes(ref, sem):
+        pltpu.make_async_copy(ref, ref, sem).wait()
+
     def turn(arr, j):
-        in_copy(arr, j).wait()
+        if j == 0:
+            in_copy(arr, j).wait()
+        elif arr == 0:
+            await_bytes(inputs.at[:, :, columns(j)], in_sem.at[2 + j])
         for at in range(groups[j][0], groups[j][1], LANES):
-            turned[arr][pl.ds(at, LANES), :] = held[arr][:, pl.ds(at, LANES)].T
+            turned[arr][pl.ds(at, LANES), :] = inputs[arr, :, pl.ds(at, LANES)].T
 
     def piece(arr, j, src):
-        return (k_all, q_all, v_all)[arr].at[j, src, pl.ds(0, HEAD_DIM), :]
+        if arr == 2:
+            return v_all.at[j, src, pl.ds(0, HEAD_DIM), :]
+        return kq_all.at[arr, j, src]
+
+    def landed(arr, j):
+        return move_recv.at[local + j if arr == 2 else j]
 
     def rows_of(arr, j, dst):
         at = pl.multiple_of((j * nz + dst) * HEAD_DIM, 16)
@@ -92,8 +120,8 @@
         return pltpu.make_async_remote_copy(
             src_ref=rows_of(arr, j, dst),
             dst_ref=piece(arr, j, z),
-            send_sem=move_send.at[arr],
-            recv_sem=move_recv.at[arr, j],
+            send_sem=move_send.at[arr // 2],
+            recv_sem=landed(arr, j),
             device_id={"seq": dst},
             device_id_type=MESH,
         )
@@ -101,7 +129,7 @@
     def send_piece(arr, j):
         for t in range(nz - 1):
             remote(arr, j, t).start()
-        pltpu.make_async_copy(rows_of(arr, j, z), piece(arr, j, z), move_recv.at[arr, j]).start()
+        pltpu.make_async_copy(rows_of(arr, j, z), piece(arr, j, z), landed(arr, j)).start()
 
     def text_copy(t):
         return pltpu.make_async_remote_copy(
@@ -122,9 +150,6 @@
             device_id={"batch": lax.rem(b + r, nb)},
             device_id_type=MESH,
         )
-
-    def await_bytes(ref, sem):
-        pltpu.make_async_copy(ref, ref, sem).wait()
 
     for j in range(local):
         for arr in range(3):
@@ -141,31 +166,29 @@
     row_block = min(128, tok)
     chunks = tok // row_block
 
-    def o_rows(j, src, c):
-        at = pl.multiple_of(src * HEAD_DIM, 16)
-        return att_t.at[j, pl.ds(at, HEAD_DIM), pl.ds(c * row_block, row_block)]
-
-    def o_copy(j, t, c):
+    far = nz - half
+    last = local - 1
+    middle = (z == half - 1) | (z == half)
+
+    def slot(src, dst):
+        return lax.rem(jnp.where(dst < half, nz - 1 - src, src) + half, nz)
+
+    def o_copy(j, t, at, sem):
         dst = partner(t)
+        rows = pl.ds(pl.multiple_of(slot(z, dst) * HEAD_DIM, 16), HEAD_DIM)
         return pltpu.make_async_remote_copy(
-            src_ref=o_send.at[j, dst, :, pl.ds(c * row_block, row_block)],
-            dst_ref=o_rows(j, z, c),
+            src_ref=o_send.at[j, dst, :, at],
+            dst_ref=att_t.at[j, rows, at],
             send_sem=o_ssem,
-            recv_sem=o_rsem.at[j, c],
+            recv_sem=o_rsem.at[sem],
             device_id={"seq": dst},
             device_id_type=MESH,
         )
 
-    def o_arrive(j, c):
-        here = pl.ds(c * row_block, row_block)
-        await_bytes(att_t.at[j, pl.ds(0, (nz - 1) * HEAD_DIM), here], o_rsem.at[j, c])
-
-    far = nz - half
+    def block(c):
+        return pl.ds(c * row_block, row_block)
+
     scale = HEAD_DIM ** (-0.5) * 1.4426950408889634
-
-    def arrive(arr, j):
-        ref = (k_all, q_all, v_all)[arr].at[j, :, pl.ds(0, HEAD_DIM), :]
-        await_bytes(ref, move_recv.at[arr, j])
 
     def partner_at(t):
         crossing = jnp.where(t < nz - half, 1, 0)
@@ -178,18 +201,17 @@
 
         @pl.when(t == 0)
         def _():
-            arrive(0, j)
+            await_bytes(kq_all.at[:, j], landed(0, j))
             for src in range(nz):
-                k_rows[pl.ds(src * tok, tok), :] = k_all[j, src].T
-            arrive(1, j)
+                k_rows[pl.ds(src * tok, tok), :] = kq_all[0, j, src].T
 
         dst = partner_at(t)
-        s = jnp.dot(k_rows[...], q_all[j, dst], preferred_element_type=jnp.float32)
+        s = jnp.dot(k_rows[...], kq_all[1, j, dst], preferred_element_type=jnp.float32)
         p = jnp.exp2((s - jnp.max(s, axis=0, keepdims=True)) * scale).astype(jnp.bfloat16)
 
         @pl.when(t == 0)
         def _():
-            arrive(2, j)
+            await_bytes(v_all.at[j, :, pl.ds(0, HEAD_DIM), :], landed(2, j))
 
         out = jnp.zeros((HEAD_DIM + ONES_ROWS, tok), jnp.float32)
         for src in range(nz):
@@ -204,22 +226,29 @@
             def _():
                 o_send[j, partner(at)] = mixed
 
-                @pl.when((j < local - 1) | (at >= far))
-                def _():
-                    for c in range(chunks):
-                        o_copy(j, at, c).start()
+                if at >= far:
+                    o_copy(j, at, pl.ds(0, tok), j).start()
+                else:
+
+                    @pl.when(jnp.logical_not(middle))
+                    def _():
+                        o_copy(j, at, pl.ds(0, tok), j).start()
+
+                    @pl.when(middle & (j < last))
+                    def _():
+                        o_copy(j, at, pl.ds(0, tok), local + j).start()
 
                 if at == far - 1:
 
-                    @pl.when(j == local - 1)
+                    @pl.when(middle & (j == last))
                     def _():
                         for c in range(chunks):
-                            for near in range(far):
-                                o_copy(j, near, c).start()
+                            for to in reversed(range(far)):
+                                o_copy(j, to, block(c), local + last + c).start()
 
         @pl.when(t == nz - 1)
         def _():
-            att_t[j, pl.ds(pl.multiple_of(z * HEAD_DIM, 16), HEAD_DIM), :] = mixed
+            att_t[j, pl.ds(pl.multiple_of(slot(z, z) * HEAD_DIM, 16), HEAD_DIM), :] = mixed
 
         @pl.when((j == 0) & (t == nz - 1))
         def _():
@@ -233,31 +262,46 @@
 
     for copy in loads:
         copy.wait()
+    await_bytes(w_v, w_sem)
+    rows = lax.broadcasted_iota(jnp.int32, (nb, LANES), 0)
+    lanes = lax.broadcasted_iota(jnp.int32, (nb, LANES), 1)
+    matching = jnp.zeros((nb, LANES), jnp.int32)
+    for i in range(nb):
+        matching = jnp.where(rows == i, labels_ref[i], matching)
+    match_out[...] = matching
     depth = nz * HEAD_DIM
 
-    def product(j, c):
+    def product(j, first, count, at):
         return jnp.dot(
-            att_t[j, :, pl.ds(c * row_block, row_block)].T,
-            w_v[pl.ds(j * depth, depth), :],
+            att_t[j, pl.ds(first * HEAD_DIM, count * HEAD_DIM), at].T,
+            w_v[pl.ds(j * depth + first * HEAD_DIM, count * HEAD_DIM), :],
             preferred_element_type=jnp.float32,
         )
 
-    for j in range(local - 1):
-        for c in range(chunks):
-            here = pl.ds(c * row_block, row_block)
-            o_arrive(j, c)
+    halves = [pl.ds(at, tok // 2) for at in range(0, tok, tok // 2)]
+    for j in range(local):
+        if nz > 2:
+            await_bytes(att_t.at[j, pl.ds(0, (nz - 2) * HEAD_DIM)], o_rsem.at[j])
+        for here in halves:
             old = res_v[here, :].astype(jnp.float32) if j == 0 else acc[here, :]
-            acc[here, :] = old + product(j, c)
+            acc[here, :] = old + product(j, 0, nz - 1, here)
+    for j in range(last):
+        await_bytes(att_t.at[j, pl.ds(0, HEAD_DIM)], o_rsem.at[local + j])
+        for here in halves:
+            acc[here, :] += product(j, nz - 1, 1, here)
     await_bytes(text_all.at[pl.ds(0, nb - 1)], wide_rsem)
+
+    def hid_copy(c):
+        return pltpu.make_async_copy(hid_v.at[block(c), :], hid_out.at[0, block(c), :], hid_sem)
 
     pool = jnp.zeros((1, features), jnp.float32)
     for c in range(chunks):
-        here = pl.ds(c * row_block, row_block)
-        o_arrive(local - 1, c)
-        old = res_v[here, :].astype(jnp.float32) if local == 1 else acc[here, :]
-        summed = old + product(local - 1, c)
+        here = block(c)
+        await_bytes(att_t.at[last, pl.ds(0, HEAD_DIM), here], o_rsem.at[local + last + c])
+        summed = acc[here, :] + product(last, nz - 1, 1, here)
         hid_v[here, :] = summed.astype(jnp.bfloat16)
-        pltpu.make_async_copy(hid_v.at[here, :], hid_out.at[0, here, :], hid_sem).start()
+        if c < chunks - 1:
+            hid_copy(c).start()
         centred = summed - jnp.mean(summed, axis=-1, keepdims=True)
         variance = jnp.mean(centred * centred, axis=-1, keepdims=True)
         pool += jnp.sum(centred * lax.rsqrt(variance + 1e-05), axis=0, keepdims=True)
@@ -276,6 +320,7 @@
 
     for t in range(nz - 1):
         pool_copy(t).start()
+    hid_copy(chunks - 1).start()
     await_bytes(pool_all.at[pl.ds(0, nz - 1)], pool_rsem)
     pooled = pool_all[0]
     for src in range(1, nz):
@@ -299,8 +344,6 @@
             texts * embed[:, src * cols:(src + 1) * cols], axis=1, keepdims=True
         )
     squares = jnp.sum(embed * embed, axis=1, keepdims=True)
-    rows = lax.broadcasted_iota(jnp.int32, (nb, LANES), 0)
-    lanes = lax.broadcasted_iota(jnp.int32, (nb, LANES), 1)
     row = jnp.sum(jnp.where(rows == lanes, products, 0.0), axis=0, keepdims=True)
     row_all[b] = jnp.where(lanes[:1] == nb, squares, row)
 
@@ -317,8 +360,8 @@
     for r in range(1, nb):
         row_copy(r).start()
 
-    for arr in range(3):
-        await_bytes(k_all.at[:, pl.ds(0, nz - 1)], move_send.at[arr])
+    await_bytes(kq_all.at[:, :, pl.ds(0, nz - 1)], move_send.at[0])
+    await_bytes(o_send.at[:, pl.ds(0, nz - 1)], move_send.at[1])
     await_bytes(o_send.at[:, pl.ds(0, nz - 1)], o_ssem)
     await_bytes(text_all.at[b, pl.ds(0, nz - 1)], text_ssem)
     await_bytes(text_all.at[pl.ds(0, nb - 1)], wide_ssem)
@@ -329,8 +372,10 @@
     await_bytes(row_all.at[pl.ds(0, nb - 1)], row_ssem)
 
 
-def loss_kernel(nb, hid_ref, row_ref, labels_ref, hid_out, img_ref, txt_ref, sem):
-    store = pltpu.make_async_copy(hid_ref, hid_out, sem)
+def loss_kernel(
+    nb, hid_ref, row_ref, match_ref, hid_out, img_out, txt_out, img_ref, txt_ref, hid_sem, loss_sem
+):
+    store = pltpu.make_async_copy(hid_ref, hid_out, hid_sem)
     store.start()
     b = lax.axis_index("batch")
     rows = lax.broadcasted_iota(jnp.int32, (nb, LANES), 0)
@@ -339,10 +384,7 @@
     norm = jnp.sum(jnp.where(lanes == nb, total, 0.0), axis=1, keepdims=True)
     logits = total * lax.rsqrt(norm + 1e-06)
     valid = lanes < nb
-    matching = jnp.zeros((nb, LANES), jnp.int32)
-    for i in range(nb):
-        matching = jnp.where(rows == i, labels_ref[i], matching)
-    picked = jnp.where(matching == lanes, logits, 0.0)
+    picked = jnp.where(match_ref[...] == lanes, logits, 0.0)
     shown = jnp.where(valid, logits, -3e38)
     top = jnp.max(shown, axis=1, keepdims=True)
     image = (
@@ -358,7 +400,13 @@
     )
     img_ref[0] = jnp.sum(jnp.where((rows == b) & (lanes == 0), image, 0.0))
     txt_ref[0] = jnp.sum(jnp.where((rows == 0) & (lanes == b), text, 0.0))
+    image_store = pltpu.make_async_copy(img_ref, img_out, loss_sem.at[0])
+    text_store = pltpu.make_async_copy(txt_ref, txt_out, loss_sem.at[1])
+    image_store.start()
+    text_store.start()
     store.wait()
+    image_store.wait()
+    text_store.wait()
 
 
 def fused(queries, keys, values, residual_in, w_out, ln_gain, w_proj, texts, labels):
@@ -369,24 +417,29 @@
     cols = texts.shape[1]
     bf16, f32 = jnp.bfloat16, jnp.float32
     anywhere = pl.BlockSpec(memory_space=pl.ANY)
-    smem = pl.BlockSpec(memory_space=pltpu.SMEM)
     dma = pltpu.SemaphoreType.DMA
     wide = pltpu.VMEM((tok, features), bf16)
     tall = pltpu.VMEM((features, tok), bf16)
     hidden_shape = jax.ShapeDtypeStruct((1, tok, features), bf16)
-    hidden, rows = pl.pallas_call(
+    loss_shape = jax.ShapeDtypeStruct((1,), f32)
+    hbm, vmem = pl.BlockSpec(memory_space=pltpu.HBM), pl.BlockSpec(memory_space=pltpu.VMEM)
+    hidden, rows, matching = pl.pallas_call(
         functools.partial(fused_kernel, nb, nz),
-        out_shape=(hidden_shape, jax.ShapeDtypeStruct((nb, LANES), f32)),
-        in_specs=[pl.BlockSpec(memory_space=pltpu.HBM)] * 8,
-        out_specs=(anywhere, pl.BlockSpec(memory_space=pltpu.VMEM)),
+        out_shape=(
+            hidden_shape,
+            jax.ShapeDtypeStruct((nb, LANES), f32),
+            jax.ShapeDtypeStruct((nb, LANES), jnp.int32),
+        ),
+        in_specs=[hbm] * 9,
+        out_specs=(anywhere, vmem, vmem),
         scratch_shapes=[
-            wide, wide, wide, tall, tall, tall,
-            pltpu.VMEM((local, nz, HEAD_DIM, tok), bf16),
-            pltpu.VMEM((local, nz, HEAD_DIM, tok), bf16),
+            pltpu.VMEM((3, tok, features), bf16), tall, tall, tall,
+            pltpu.VMEM((2, local, nz, HEAD_DIM, tok), bf16),
             pltpu.VMEM((local, nz, HEAD_DIM + ONES_ROWS, tok), bf16),
             pltpu.VMEM((nz * tok, HEAD_DIM), bf16),
             pltpu.VMEM((features,), f32),
             pltpu.VMEM((1, cols), f32),
+            pltpu.SMEM(labels.shape, jnp.int32),
             pltpu.VMEM((local, nz, HEAD_DIM, tok), bf16),
             pltpu.VMEM((local, nz * HEAD_DIM, tok), bf16),
             pltpu.VMEM((features, features), bf16),
@@ -397,9 +450,9 @@
             pltpu.VMEM((nb, nz, 1, cols), f32),
             pltpu.VMEM((nz, 1, features), f32),
             pltpu.VMEM((nb, 1, LANES), f32),
-            dma((3, local)), dma((5,)),
-            dma((3,)), dma((3, local)),
-            dma, dma((local, chunks)),
+            dma((2 + local,)), dma((5,)), dma,
+            dma((2,)), dma((2 * local,)),
+            dma, dma((2 * local - 1 + chunks,)),
             dma, dma, dma, dma, dma, dma, dma, dma, dma,
         ],
         compiler_params=pltpu.CompilerParams(
@@ -407,18 +460,16 @@
         ),
     )(
         *(pltpu.with_memory_space_constraint(x, pltpu.HBM) for x in (queries, keys, values, residual_in, w_out, ln_gain, w_proj,
-        texts))
+        texts, labels))
     )
     return pl.pallas_call(
         functools.partial(loss_kernel, nb),
-        out_shape=(
-            hidden_shape, jax.ShapeDtypeStruct((1,), f32), jax.ShapeDtypeStruct((1,), f32),
-        ),
-        in_specs=[anywhere, pl.BlockSpec(memory_space=pltpu.VMEM), smem],
-        out_specs=(pl.BlockSpec(memory_space=pltpu.HBM), smem, smem),
-        scratch_shapes=[dma],
+        out_shape=(hidden_shape, loss_shape, loss_shape),
+        in_specs=[anywhere, vmem, vmem],
+        out_specs=(hbm, hbm, hbm),
+        scratch_shapes=[pltpu.SMEM((1,), f32), pltpu.SMEM((1,), f32), dma, dma((2,))],
         compiler_params=pltpu.CompilerParams(vmem_limit_bytes=4 * 1024 * 1024),
-    )(hidden, rows, labels)
+    )(hidden, rows, matching)
 
 
 def row_lse(logits, axis):

time: 132 us -> 130 us (0.985)
  Pallas kernels: 131 us -> 129 us
where the time goes in v2:
time: 130 us
  Pallas kernels  129 us (99%)
    pallas_call x1, Pallas kernels, fused(): pl.pallas_call(functools.partial(fused_kernel, nb, nz), out_shape=(hidden...  128 us

profile of v2, /device:TPU:0, one launch (start us, length us, event | category | flops | bytes accessed | tf_op | source)
XLA Modules:
  0.0 129.9 jit_solution(13916940013866826048)
XLA Ops:
  0.6 128.1 %shard_map.112 = (bf16[1,512,1280]{2,1,0:T(8,128)(2,1)S(1)}, f32[8,128]{1,0:T(8,128)S(1)}, s32[8,128]{1,0:T(8,128)S(1)}) custom-call(bf16[1,512,1280]{2,1,0:T(8,128)(2,1)} %q_hbm.1, bf16[1,512,1280]{2,1,0:T(8,128)(2,1)} %k_hbm.1, bf16[1,512,1280]{2,1,0:T(8,128)(2,1)} %v_hbm.1, bf16[1,512,1280]{2,1,0:T(8,128)(2,1)} %res_hbm.1, bf16[1280,1280]{1,0:T(8,128)(2,1)} %w_hbm.1, ...), custom_call_target="tpu_custom_call" | custom-call | tf_op jit(solution)/shard_map/pallas_call | solution.py:426
  128.8 1.1 shard_map.113

commit v3 on v2

--- a/solution.py
+++ b/solution.py
@@ -20,7 +20,7 @@
     q_hbm, k_hbm, v_hbm, res_hbm, w_hbm, gain_hbm, wproj_hbm, texts_hbm, labels_hbm,
     hid_out, row_out, match_out,
     inputs, k_t, q_t, v_t, kq_all, v_all, k_rows,
-    gain_ref, texts_ref, labels_ref, o_send, att_t, w_v, res_v, acc, hid_v, wproj_v, text_all, pool_all, row_all,
+    gain_ref, texts_ref, labels_ref, o_send, att_t, w_v, res_v, acc, hid_v, wproj_v, text_all, pool_send, pool_all, row_all,
     in_sem, load_sem, w_sem, move_send, move_recv, o_ssem, o_rsem,
     text_ssem, text_rsem, wide_ssem, wide_rsem, pool_ssem, pool_rsem, row_ssem, row_rsem, hid_sem,
 ):
@@ -60,6 +60,14 @@
     for r in range(1, nb):
         pl.semaphore_signal(
             barrier, inc=1, device_id={"batch": lax.rem(b + r, nb)}, device_id_type=MESH
+        )
+    odd = lax.rem(b, 2)
+    for t in range(nz - 1):
+        pl.semaphore_signal(
+            barrier,
+            inc=1,
+            device_id={"batch": b + 1 - 2 * odd, "seq": partner(t)},
+            device_id_type=MESH,
         )
     loads = [
         pltpu.make_async_copy(src, dst, load_sem.at[i])
@@ -155,7 +163,7 @@
         for arr in range(3):
             turn(arr, j)
             if j == arr == 0:
-                pl.semaphore_wait(barrier, nz - 1 + nb - 1)
+                pl.semaphore_wait(barrier, 2 * (nz - 1) + nb - 1)
             send_piece(arr, j)
             if j == arr == 0:
                 text_load.wait()
@@ -306,70 +314,91 @@
         variance = jnp.mean(centred * centred, axis=-1, keepdims=True)
         pool += jnp.sum(centred * lax.rsqrt(variance + 1e-05), axis=0, keepdims=True)
 
-    pool_all[z] = pool * gain_ref[...].reshape(1, features)
-
-    def pool_copy(t):
+    pool_send[...] = pool * gain_ref[...].reshape(1, features)
+    head = b + 1 - odd
+
+    def pool_copy(to):
         return pltpu.make_async_remote_copy(
-            src_ref=pool_all.at[z],
-            dst_ref=pool_all.at[z],
+            src_ref=pool_send,
+            dst_ref=pool_all.at[odd * nz + z],
             send_sem=pool_ssem,
             recv_sem=pool_rsem,
-            device_id={"seq": partner(t)},
+            device_id={"batch": head, "seq": to},
             device_id_type=MESH,
         )
 
     for t in range(nz - 1):
-        pool_copy(t).start()
+        pool_copy(partner(t)).start()
+
+    @pl.when(odd == 0)
+    def _():
+        pool_copy(z).start()
+
     hid_copy(chunks - 1).start()
-    await_bytes(pool_all.at[pl.ds(0, nz - 1)], pool_rsem)
-    pooled = pool_all[0]
-    for src in range(1, nz):
-        pooled = pooled + pool_all[src]
-    pooled = pooled / (nz * tok)
-
-    high = pooled.astype(jnp.bfloat16).astype(jnp.float32)
-    middle = (pooled - high).astype(jnp.bfloat16).astype(jnp.float32)
-    low = pooled - high - middle
-    row_id = lax.broadcasted_iota(jnp.int32, (16, features), 0)
-    parts = jnp.where(
-        row_id == 0, high, jnp.where(row_id == 1, middle, jnp.where(row_id == 2, low, 0.0))
-    ).astype(jnp.bfloat16)
-    embed = jnp.sum(
-        jnp.dot(parts, wproj_v[...], preferred_element_type=jnp.float32), axis=0, keepdims=True
-    )
-    products = jnp.zeros((nb, 1), jnp.float32)
-    for src in range(nz):
-        texts = text_all[:, src].reshape(nb, cols)
-        products += jnp.sum(
-            texts * embed[:, src * cols:(src + 1) * cols], axis=1, keepdims=True
-        )
-    squares = jnp.sum(embed * embed, axis=1, keepdims=True)
-    row = jnp.sum(jnp.where(rows == lanes, products, 0.0), axis=0, keepdims=True)
-    row_all[b] = jnp.where(lanes[:1] == nb, squares, row)
 
     def row_copy(r):
+        pair = pl.ds(b - 1, 2)
         return pltpu.make_async_remote_copy(
-            src_ref=row_all.at[b],
-            dst_ref=row_all.at[b],
+            src_ref=row_all.at[pair],
+            dst_ref=row_all.at[pair],
             send_sem=row_ssem,
             recv_sem=row_rsem,
             device_id={"batch": lax.rem(b + r, nb)},
             device_id_type=MESH,
         )
 
-    for r in range(1, nb):
-        row_copy(r).start()
+    @pl.when(odd == 1)
+    def _():
+        await_bytes(pool_all.at[pl.ds(0, 2 * nz - 1)], pool_rsem)
+        row_id = lax.broadcasted_iota(jnp.int32, (16, features), 0)
+        parts = jnp.zeros((16, features), jnp.float32)
+        for image in range(2):
+            pooled = pool_send[...] if image else pool_all[0]
+            for at in range(1, nz):
+                src = nz + lax.rem(z + at, nz) if image else at
+                pooled = pooled + pool_all[src]
+            pooled = pooled / (nz * tok)
+            high = pooled.astype(jnp.bfloat16).astype(jnp.float32)
+            middle_part = (pooled - high).astype(jnp.bfloat16).astype(jnp.float32)
+            low = pooled - high - middle_part
+            for place, part in enumerate((high, middle_part, low)):
+                parts = jnp.where(row_id == 8 * image + place, part, parts)
+        embeds = jnp.dot(
+            parts.astype(jnp.bfloat16), wproj_v[...], preferred_element_type=jnp.float32
+        )
+        for image in range(2):
+            embed = jnp.sum(embeds[8 * image:8 * image + 8], axis=0, keepdims=True)
+            products = jnp.zeros((nb, 1), jnp.float32)
+            for src in range(nz):
+                texts = text_all[:, src].reshape(nb, cols)
+                products += jnp.sum(
+                    texts * embed[:, src * cols:(src + 1) * cols], axis=1, keepdims=True
+                )
+            squares = jnp.sum(embed * embed, axis=1, keepdims=True)
+            row = jnp.sum(jnp.where(rows == lanes, products, 0.0), axis=0, keepdims=True)
+            row_all[b - 1 + image] = jnp.where(lanes[:1] == nb, squares, row)
+        for r in range(1, nb):
+            row_copy(r).start()
 
     await_bytes(kq_all.at[:, :, pl.ds(0, nz - 1)], move_send.at[0])
     await_bytes(o_send.at[:, pl.ds(0, nz - 1)], move_send.at[1])
     await_bytes(o_send.at[:, pl.ds(0, nz - 1)], o_ssem)
     await_bytes(text_all.at[b, pl.ds(0, nz - 1)], text_ssem)
     await_bytes(text_all.at[pl.ds(0, nb - 1)], wide_ssem)
-    await_bytes(pool_all.at[pl.ds(0, nz - 1)], pool_ssem)
     pltpu.make_async_copy(hid_v, hid_out.at[0], hid_sem).wait()
-    await_bytes(row_all.at[pl.ds(0, nb - 1)], row_rsem)
-    row_out[...] = row_all[...].reshape(nb, LANES)
-    await_bytes(row_all.at[pl.ds(0, nb - 1)], row_ssem)
+
+    @pl.when(odd == 0)
+    def _():
+        await_bytes(pool_all.at[pl.ds(0, nz)], pool_ssem)
+        await_bytes(row_all.at[pl.ds(0, nb)], row_rsem)
+
+    @pl.when(odd == 1)
+    def _():
+        await_bytes(pool_all.at[pl.ds(0, nz - 1)], pool_ssem)
+        await_bytes(row_all.at[pl.ds(0, nb - 2)], row_rsem)
+        await_bytes(row_all.at[pl.ds(0, 2 * (nb - 1))], row_ssem)
+
+    row_out[...] = row_all[pl.ds(0, nb)].reshape(nb, LANES)
 
 
 def loss_kernel(
@@ -448,8 +477,9 @@
             wide,
             pltpu.VMEM(w_proj.shape, bf16),
             pltpu.VMEM((nb, nz, 1, cols), f32),
-            pltpu.VMEM((nz, 1, features), f32),
-            pltpu.VMEM((nb, 1, LANES), f32),
+            pltpu.VMEM((1, features), f32),
+            pltpu.VMEM((2 * nz, 1, features), f32),
+            pltpu.VMEM((2 * nb, 1, LANES), f32),
             dma((2 + local,)), dma((5,)), dma,
             dma((2,)), dma((2 * local,)),
             dma, dma((2 * local - 1 + chunks,)),

time: 130 us -> 130 us (level)
  no operation moved by 1% of the time
where the time goes in v3:
time: 130 us; the launch traced here: 129 us
  Pallas kernels  129 us (99%)
    pallas_call x1, Pallas kernels, fused(): pl.pallas_call(functools.partial(fused_kernel, nb, nz), out_shape=(hidden...  128 us

profile of v3, /device:TPU:0, one launch (start us, length us, event | category | flops | bytes accessed | tf_op | source)
XLA Modules:
  0.0 129.5 jit_solution(9036299794061440627)
XLA Ops:
  0.6 127.7 %shard_map.112 = (bf16[1,512,1280]{2,1,0:T(8,128)(2,1)S(1)}, f32[8,128]{1,0:T(8,128)S(1)}, s32[8,128]{1,0:T(8,128)S(1)}) custom-call(bf16[1,512,1280]{2,1,0:T(8,128)(2,1)} %q_hbm.1, bf16[1,512,1280]{2,1,0:T(8,128)(2,1)} %k_hbm.1, bf16[1,512,1280]{2,1,0:T(8,128)(2,1)} %v_hbm.1, bf16[1,512,1280]{2,1,0:T(8,128)(2,1)} %res_hbm.1, bf16[1280,1280]{1,0:T(8,128)(2,1)} %w_hbm.1, ...), custom_call_target="tpu_custom_call" | custom-call | tf_op jit(solution)/shard_map/pallas_call | solution.py:455
  128.4 1.1 shard_map.113
